TPU v7x, 32 devices: a whole 2x2x4 slice. The times are simulated.
32 devices in a mesh: grp: 2 (over y), col: 4 (over z), row: 2 (over x), dir: 2 (over core).
Axes of the slice: x: 2, y: 2, z: 4, core: 2. Of those that a mesh axis runs over, the one named last changes fastest.
Arguments:
- slopes_in: bfloat16 [512, 8192], P(None, ('grp', 'col')), parts along dimension 1, may hold values from -6 to 6
- basis_left: bfloat16 [12, 16, 256, 256], P(('row', 'dir'), 'col'), may hold values from -0.09375 to 0.09375
- basis_right: bfloat16 [12, 16, 256, 256], P(('row', 'dir'), 'col'), may hold values from -0.375 to 0.375
- rank_blocks: int32 [12, 16], P(('row', 'dir'), 'col'), may hold values from 1 to 4
- tile_owner: int32 [16], replicated, may hold values from 0 to 15, each once
- footprint: int32 [4, 4, 4, 2048], P(('row', 'dir')), may hold values from 0 to 767
- trace_weight: float32 [4, 4, 4, 2048], P(('row', 'dir')), may hold values from 0 to 0.5
- fitting: bfloat16 [2048, 4096], P(None, 'col'), may hold values from -0.125 to 0.125
Outputs:
- commands: bfloat16 [4, 1024, 4096], P(('row', 'dir'), 'grp', 'col'), parts along dimension 1
There are 2 independent parts, one for each index of `grp`. A program takes and returns all parts, laid end to end along the dimension named above; an argument that names none is the same for every part. Nothing has to cross between parts.
Inputs may be any that keep to these rules, and one draw needn't show every extreme that they name: rank_blocks[i, k] is the number of leading blocks of 64 columns of tile (i, k) that are live. `tile_owner`: each slope block appears in exactly one tile slot. `footprint`: indices into one layer's points.
All inputs are finite; a program needn't handle non-finite values.
Results may differ from a plain program's by a relative error of at most 0.0064.
Values may be sent and summed in bfloat16 or wider, within the bound.
No kernel may reach another device: no remote copies, remote signals or barrier semaphores. Data moves between devices by JAX's collectives and lax.ppermute only.
A program may use at most 128 MiB of HBM per device.

v0:
```python
import jax
import jax.numpy as jnp
from jax import lax
from jax.sharding import PartitionSpec as P

RB = 64


def shards(
    slopes_in, basis_left, basis_right, rank_blocks, tile_owner, footprint, trace_weight, fitting
):
    frames = slopes_in.shape[0]
    tile_size = basis_left.shape[2]
    rows_here = basis_left.shape[0]
    slots_here = basis_left.shape[1]
    rank_cols = basis_left.shape[3]
    owners = lax.dynamic_slice_in_dim(tile_owner, lax.axis_index("col") * slots_here, slots_here, 0)
    share = frames // lax.axis_size(("row", "dir"))
    mine = lax.dynamic_slice_in_dim(slopes_in, lax.axis_index(("row", "dir")) * share, share, 0)
    partial_value = lax.all_gather(mine, "col", axis=1, tiled=True)
    picked = jnp.take(partial_value.reshape(share, -1, tile_size), owners, axis=1)
    chosen = lax.all_gather(picked, ("row", "dir"), axis=0, tiled=True)
    columns = jnp.arange(rank_cols, dtype=jnp.int32) // RB
    live = columns[None, None, None, :] < rank_blocks[:, :, None, None]
    frame_share = frames // lax.axis_size("col")
    coeffs = jnp.einsum("fkn,iknr->ikfr", chosen, basis_right, preferred_element_type=jnp.float32)
    coeffs = jnp.where(live, coeffs, 0.0).astype(jnp.bfloat16)
    summed = jnp.einsum("ikfr,iknr->fin", coeffs, basis_left, preferred_element_type=jnp.float32)
    layer_block = lax.psum_scatter(
        summed.reshape(lax.axis_size("col") * frame_share, rows_here * tile_size),
        "col",
        scatter_dimension=0,
        tiled=True,
    ).astype(jnp.bfloat16)
    layers = lax.all_gather(layer_block, ("row", "dir"), axis=1, tiled=True)
    layer_count = footprint.shape[1]
    pupil_count = footprint.shape[3]
    per_layer = layers.shape[1] // layer_count
    shifts = (jnp.arange(layer_count, dtype=jnp.int32) * per_layer)[:, None, None]
    flat = (footprint[0] + shifts).reshape(-1)
    values = (
        jnp.take(layers, flat, axis=1)
        .astype(jnp.float32)
        .reshape(frame_share, layer_count, 4, pupil_count)
    )
    pupil = jnp.sum(values * trace_weight[0][None], axis=(1, 2)).astype(jnp.bfloat16)
    commands = jnp.dot(
        lax.all_gather(pupil, "col", axis=0, tiled=True),
        fitting,
        preferred_element_type=jnp.float32,
    )
    return commands.astype(jnp.bfloat16)[None]


def solution(mesh):
    placed = (
        P(None, ("grp", "col")),
        P(("row", "dir"), "col", None, None),
        P(("row", "dir"), "col", None, None),
        P(("row", "dir"), "col"),
        P(),
        P(("row", "dir"), None, None, None),
        P(("row", "dir"), None, None, None),
        P(None, "col"),
    )
    return jax.shard_map(
        shards,
        mesh=mesh,
        in_specs=placed,
        out_specs=P(("row", "dir"), "grp", "col"),
        check_vma=False,
    )
```

profile of v0, /device:TPU:0, one launch (start us, length us, event | category | flops | bytes accessed | tf_op | source)
XLA Modules:
  0.0 293.8 jit_solution(6185712206535708235)
XLA Ops:
  6.5 0.0 copy-start
  6.5 0.0 all-gather.4.cloned.1.call-start
  6.6 1.1 constant_dynamic-slice_fusion
  7.7 0.8 copy.14
  8.5 0.0 all-gather.4.cloned.1.call-update
  8.5 0.0 all-gather.6.cloned.1.call-start
  8.6 0.7 compare_and_fusion.1
  9.3 30.3 %all-gather.4.cloned.1.call-done = bf16[128,4096]{0,1:T(8,128)(2,1)} async-done(((bf16[128,1024]{0,1:T(8,128)(2,1)}), bf16[128,4096]{0,1:T(8,128)(2,1)}) %all-gather.4.cloned.1.call-update) | async-done | bytes 1048592 | tf_op jit(solution)/shard_map/all_gather | solution.py:20
  39.6 1.5 copy.12
  41.1 0.6 gather_fusion
  41.7 0.8 select_bitcast_fusion
  42.5 0.0 all-gather.6.cloned.1.call-update
  42.5 0.0 reduce-scatter.2.cloned.1.call-start
  42.6 0.1 add.67
  42.7 0.2 add.75
  42.9 0.2 squeeze.6
  43.1 0.0 copy-done.3
  43.1 0.1 broadcast_compare_fusion
  43.1 15.6 %all-gather.6.cloned.1.call-done = bf16[512,4,256]{2,0,1:T(8,128)(2,1)} async-done(((bf16[128,4,256]{2,0,1:T(8,128)(2,1)}), bf16[512,4,256]{2,0,1:T(8,128)(2,1)}) %all-gather.6.cloned.1.call-update) | async-done | bytes 1048592 | tf_op jit(solution)/shard_map/all_gather | solution.py:22
  58.8 4.7 %fusion.1 = f32[3,512,256,1]{1,2,3,0:T(8,128)} fusion(bf16[3,4,256,256]{3,2,1,0:T(8,128)(2,1)S(1)} %copy-done, pred[3,4,256]{2,1,0:T(4,128)(4,1)S(1)} %broadcast_compare_fusion, bf16[3,4,256,256]{3,2,1,0:T(8,128)(2,1)} %param.10, bf16[512,4,256]{2,0,1:T(8,128)(2,1)} %all-gather.6.cloned.1.call-done), kind=kOutput, calls=%fused_computation.5 | convolution fusion | flops 1613758464 | bytes 5770240 | tf_op jit(solution)/shard_map/ikfr,iknr->fin/dot_general | solution.py:28
  63.4 0.0 reduce-scatter.2.cloned.1.call-update
  63.5 0.0 all-gather.8.cloned.1.call-start
  63.5 0.2 compare_select_fusion
  63.7 0.2 compare_and_fusion
  63.9 35.2 %reduce-scatter.2.cloned.1.call-done = f32[128,768]{0,1:T(8,128)} async-done(((f32[512,768]{0,1:T(8,128)}), f32[128,768]{0,1:T(8,128)}) %reduce-scatter.2.cloned.1.call-update) | async-done | bytes 393232 | tf_op jit(solution)/shard_map/reduce_scatter | solution.py:29
  99.1 1.0 convert_element_type.17
  100.1 8.6 %all_gather.14 = bf16[128,3072]{0,1:T(8,128)(2,1)S(1)} all-gather(bf16[128,768]{0,1:T(8,128)(2,1)S(1)} %convert_element_type.17), channel_id=1, replica_groups=mesh['grp'=2,'col'=4,'row'=2,'dir'=2] {'row','dir'}, dimensions={1}, use_global_device_ids=true | all-gather | bytes 983040 | tf_op jit(solution)/shard_map/all_gather | solution.py:35
  108.6 114.3 %gather_fusion.1 = bf16[32768,128]{1,0:T(8,128)(2,1)} fusion(bf16[128,3072]{0,1:T(8,128)(2,1)S(1)} %all_gather.14, s32[32768]{0:T(1024)S(1)} %broadcast_clamp_fusion), kind=kCustom, calls=%fused_computation.1 | custom fusion | bytes 16908288 | tf_op jit(solution)/shard_map/jit(_take)/gather | solution.py:42
  222.9 13.4 %multiply_reduce_fusion = bf16[128,2048]{0,1:T(8,128)(2,1)} fusion(f32[4,4,2048]{2,1,0:T(4,128)S(1)} %bitcast.39, bf16[128,4,4,2048]{0,3,2,1:T(8,128)(2,1)} %bitcast.35, pred[4,4,2048]{2,1,0:T(4,128)(4,1)S(1)} %compare_and_fusion), kind=kLoop, calls=%fused_computation.2 | loop fusion | flops 16515072 | bytes 9076736 | tf_op jit(solution)/shard_map/reduce_sum | solution.py:46
  236.3 0.0 all-gather.8.cloned.1.call-update
  236.3 44.8 %all-gather.8.cloned.1.call-done = bf16[512,2048]{0,1:T(8,128)(2,1)} async-done(((bf16[128,2048]{0,1:T(8,128)(2,1)}), bf16[512,2048]{0,1:T(8,128)(2,1)}) %all-gather.8.cloned.1.call-update) | async-done | bytes 2097168 | tf_op jit(solution)/shard_map/all_gather | solution.py:48
  281.2 6.1 %fusion.7 = bf16[1,512,1024]{2,1,0:T(8,128)(2,1)} fusion(bf16[512,2048]{0,1:T(8,128)(2,1)} %all-gather.8.cloned.1.call-done, bf16[2048,1024]{1,0:T(8,128)(2,1)} %param.15), kind=kOutput, calls=%fused_computation.10 | convolution fusion | flops 2148007936 | bytes 7340032 | tf_op jit(solution)/shard_map/dot_general | solution.py:47
  (10 shorter events, 0.0 us)
Async XLA Ops:
  6.5 52.2 %copy-start = (bf16[3,4,256,256]{3,2,1,0:T(8,128)(2,1)S(1)}, bf16[3,4,256,256]{3,2,1,0:T(8,128)(2,1)}, u32[]{:S(2)}) copy-start(bf16[3,4,256,256]{3,2,1,0:T(8,128)(2,1)} %param.9) | copy-start | bytes 4718596
  6.5 36.3 %copy-start.1 = (s32[1,4,4,2048]{3,2,1,0:T(4,128)S(1)}, s32[1,4,4,2048]{3,2,1,0:T(4,128)}, u32[]{:S(2)}) copy-start(s32[1,4,4,2048]{3,2,1,0:T(4,128)} %param.13) | copy-start | bytes 393220
  6.5 36.5 %copy-start.3 = (s32[3,4]{1,0:T(4,128)S(1)}, s32[3,4]{1,0:T(4,128)}, u32[]{:S(2)}) copy-start(s32[3,4]{1,0:T(4,128)} %param.11) | copy-start | bytes 148
  6.5 33.1 %all-gather.4.cloned.1.call-start = ((), (), s32[]{:S(2)}) async-start(), calls=%async_computation.1 | async-start | bytes 1310720 | tf_op jit(solution)/shard_map/all_gather | solution.py:20
  8.5 50.2 %all-gather.6.cloned.1.call-start = ((), (), s32[]{:S(2)}) async-start(), calls=%async_computation.2 | async-start | bytes 1310720 | tf_op jit(solution)/shard_map/all_gather | solution.py:22
  42.5 56.5 %reduce-scatter.2.cloned.1.call-start = ((), (), s32[]{:S(2)}) async-start(), calls=%async_computation.3 | async-start | bytes 1966080 | tf_op jit(solution)/shard_map/reduce_scatter | solution.py:29
  63.5 217.7 %all-gather.8.cloned.1.call-start = ((), (), s32[]{:S(2)}) async-start(), calls=%async_computation.4 | async-start | bytes 2621440 | tf_op jit(solution)/shard_map/all_gather | solution.py:48
  108.6 114.3 %copy-start.2 = (f32[1,4,4,2048]{3,2,1,0:T(4,128)S(1)}, f32[1,4,4,2048]{3,2,1,0:T(4,128)}, u32[]{:S(2)}) copy-start(f32[1,4,4,2048]{3,2,1,0:T(4,128)} %param.14) | copy-start | bytes 393220
Sparse Core Ops, SparseCore 0:
  8.9 30.6 all-gather.3
  42.6 16.0 all-gather.5
  63.6 35.4 reduce-scatter.1
  236.5 44.6 all-gather.7
where the time goes:
time: 294 us
  waiting for transfers between devices  126 us (43%)
  local copies, waits for them, and re-layouts  119 us (40%)
  other arithmetic  16.4 us (6%)
  between operations  13.2 us (4%)
  matrix products  10.8 us (4%)
  blocking collectives  8.58 us (3%)
    gather x1, local copies, waits for them, and re-layouts, shards(): jnp.take(layers, flat, axis=1).astype(jnp.float32)  114 us
    all_gather x1, waiting for transfers between devices, shards(): lax.all_gather(pupil, 'col', axis=0, tiled=True)  44.8 us
    reduce_scatter x1, waiting for transfers between devices, shards(): lax.psum_scatter(summed.reshape(lax.axis_size('col') * frame_share, rows_...  35.2 us
    all_gather x1, waiting for transfers between devices, shards(): partial_value = lax.all_gather(mine, 'col', axis=1, tiled=True)  30.3 us
    all_gather x1, waiting for transfers between devices, shards(): chosen = lax.all_gather(picked, ('row', 'dir'), axis=0, tiled=True)  15.6 us
    reduce_sum x1, other arithmetic, shards(): jnp.sum(values * trace_weight[0][None], axis=(1, 2)).astype(jnp.bfloat16)  13.4 us
    all_gather x1, blocking collectives, shards(): layers = lax.all_gather(layer_block, ('row', 'dir'), axis=1, tiled=True)  8.58 us
    dot_general x1, matrix products, shards(): jnp.dot(lax.all_gather(pupil, 'col', axis=0, tiled=True), fitting, prefer...  6.14 us
  transfers between devices with their start and end apart: 4, of which 4 were waited for; matrix products, arithmetic and copies ran while one was open for 1% of the time, Pallas kernels for 0%

commit v1 on v0

--- a/solution.py
+++ b/solution.py
@@ -4,6 +4,32 @@
 from jax.sharding import PartitionSpec as P
 
 RB = 64
+
+
+def ring_apply(array, axis, dim, work, out_dim):
+    peers, place, rows = (lax.axis_size(axis), lax.axis_index(axis), array.shape[dim])
+    right = [(i, (i + 1) % peers) for i in range(peers)]
+    backward = [(b, a) for a, b in right]
+    lower, upper = (lax.ppermute(array, axis, right), lax.ppermute(array, axis, backward))
+    made = work(array, place * rows)
+    length = made.shape[out_dim]
+    result = jnp.zeros(
+        (*made.shape[:out_dim], peers * length, *made.shape[out_dim + 1 :]), made.dtype
+    )
+
+    def put(result, made, owner):
+        return lax.dynamic_update_slice_in_dim(result, made, owner * length, axis=out_dim)
+
+    result = put(result, made, place)
+    for step in range(1, peers // 2 + 1):
+        below, above = ((place - step) % peers, (place + step) % peers)
+        held = (lower, upper)
+        if step < peers // 2:
+            lower, upper = (lax.ppermute(lower, axis, right), lax.ppermute(upper, axis, backward))
+        result = put(result, work(held[0], below * rows), below)
+        if 2 * step < peers:
+            result = put(result, work(held[1], above * rows), above)
+    return result
 
 
 def shards(
@@ -19,11 +45,18 @@
     mine = lax.dynamic_slice_in_dim(slopes_in, lax.axis_index(("row", "dir")) * share, share, 0)
     partial_value = lax.all_gather(mine, "col", axis=1, tiled=True)
     picked = jnp.take(partial_value.reshape(share, -1, tile_size), owners, axis=1)
-    chosen = lax.all_gather(picked, ("row", "dir"), axis=0, tiled=True)
     columns = jnp.arange(rank_cols, dtype=jnp.int32) // RB
     live = columns[None, None, None, :] < rank_blocks[:, :, None, None]
     frame_share = frames // lax.axis_size("col")
-    coeffs = jnp.einsum("fkn,iknr->ikfr", chosen, basis_right, preferred_element_type=jnp.float32)
+    coeffs = ring_apply(
+        picked,
+        ("row", "dir"),
+        0,
+        lambda own_block, offset: jnp.einsum(
+            "fkn,iknr->ikfr", own_block, basis_right, preferred_element_type=jnp.float32
+        ),
+        2,
+    )
     coeffs = jnp.where(live, coeffs, 0.0).astype(jnp.bfloat16)
     summed = jnp.einsum("ikfr,iknr->fin", coeffs, basis_left, preferred_element_type=jnp.float32)
     layer_block = lax.psum_scatter(

time: 294 us -> 288 us (0.980)
  waiting for transfers between devices: 126 us -> 118 us
    all_gather x1 -> x0, waiting for transfers between devices: 15.6 us -> none  [shards(): chosen = lax.all_gather(picked, ('row', 'dir'), axis=0, tiled=True)]
    ppermute x0 -> x3, waiting for transfers between devices: none -> 9.37 us  [the longest x1 4.65 us: ring_apply(): lax.ppermute(lower, axis, right)]
  transfers between devices with their start and end apart: 4 -> 6, of which waited for: 4 -> 6; matrix products, arithmetic and copies ran while one was open for 1% -> 2% of each run, Pallas kernels for 0% -> 0%
where the time goes in v1:
time: 288 us
  local copies, waits for them, and re-layouts  120 us (42%)
  waiting for transfers between devices  118 us (41%)
  other arithmetic  16.4 us (6%)
  between operations  13.4 us (5%)
  matrix products  9.88 us (3%)
  blocking collectives  8.6 us (3%)
    gather x1, local copies, waits for them, and re-layouts, shards(): jnp.take(layers, flat, axis=1).astype(jnp.float32)  114 us
    all_gather x1, waiting for transfers between devices, shards(): lax.all_gather(pupil, 'col', axis=0, tiled=True)  44.8 us
    reduce_scatter x1, waiting for transfers between devices, shards(): lax.psum_scatter(summed.reshape(lax.axis_size('col') * frame_share, rows_...  35.4 us
    all_gather x1, waiting for transfers between devices, shards(): partial_value = lax.all_gather(mine, 'col', axis=1, tiled=True)  28.1 us
    reduce_sum x1, other arithmetic, shards(): jnp.sum(values * trace_weight[0][None], axis=(1, 2)).astype(jnp.bfloat16)  13.4 us
    all_gather x1, blocking collectives, shards(): layers = lax.all_gather(layer_block, ('row', 'dir'), axis=1, tiled=True)  8.6 us
    dot_general x1, matrix products, shards(): jnp.dot(lax.all_gather(pupil, 'col', axis=0, tiled=True), fitting, prefer...  6.14 us
  transfers between devices with their start and end apart: 6, of which 6 were waited for; matrix products, arithmetic and copies ran while one was open for 2% of the time, Pallas kernels for 0%

profile of v1, /device:TPU:0, one launch (start us, length us, event | category | flops | bytes accessed | tf_op | source)
XLA Modules:
  0.0 287.7 jit_solution(12868500627824646772)
XLA Ops:
  6.5 1.1 constant_dynamic-slice_fusion
  7.6 0.8 copy.14
  8.6 0.1 add.93
  8.7 0.2 add.108
  8.9 1.1 squeeze.6
  10.0 0.7 compare_and_fusion.1
  10.7 0.8 broadcast_compare_fusion
  11.5 28.1 %all-gather.3.cloned.1.call-done = bf16[128,4096]{0,1:T(8,128)(2,1)} async-done(((bf16[128,1024]{0,1:T(8,128)(2,1)}), bf16[128,4096]{0,1:T(8,128)(2,1)}) %all-gather.3.cloned.1.call-update) | async-done | bytes 1048592 | tf_op jit(solution)/shard_map/all_gather | solution.py:46
  39.6 1.5 copy.12
  41.1 0.6 gather_fusion
  41.7 0.1 fusion.8
  41.8 0.1 collective-permute-start
  41.9 1.7 collective-permute-start.1
  43.6 0.3 broadcast_in_dim.43
  43.9 0.4 bitcast_dynamic-update-slice_fusion.3
  44.3 4.4 %collective-permute-done = bf16[128,4,256]{2,0,1:T(8,128)(2,1)S(1)} collective-permute-done((bf16[128,4,256]{2,0,1:T(8,128)(2,1)S(1)}, bf16[128,4,256]{2,0,1:T(8,128)(2,1)S(1)}, u32[]{:S(2)}, u32[]{:S(2)}) %collective-permute-start) | collective-permute-done | bytes 262176 | tf_op jit(solution)/shard_map/ppermute | solution.py:13
  48.7 0.4 bitcast_dynamic-update-slice_fusion.2
  49.1 0.3 collective-permute-done.1
  49.4 0.4 bitcast_dynamic-update-slice_fusion.1
  49.8 4.7 %collective-permute-done.2 = bf16[128,4,256]{2,0,1:T(8,128)(2,1)S(1)} collective-permute-done((bf16[128,4,256]{2,0,1:T(8,128)(2,1)S(1)}, bf16[128,4,256]{2,0,1:T(8,128)(2,1)S(1)}, u32[]{:S(2)}, u32[]{:S(2)}) %collective-permute-start.2) | collective-permute-done | bytes 262176 | tf_op jit(solution)/shard_map/ppermute | solution.py:28
  54.5 0.4 bitcast_dynamic-update-slice_fusion
  54.9 2.2 fusion
  57.1 0.0 all-gather.5.cloned.1.call-start
  57.1 0.2 compare_select_fusion
  57.3 0.2 compare_and_fusion
  57.5 35.4 %reduce-scatter.2.cloned.1.call-done = f32[128,768]{0,1:T(8,128)} async-done(((f32[512,768]{0,1:T(8,128)}), f32[128,768]{0,1:T(8,128)}) %reduce-scatter.2.cloned.1.call-update) | async-done | bytes 393232 | tf_op jit(solution)/shard_map/reduce_scatter | solution.py:62
  93.0 1.0 convert_element_type.17
  94.0 8.6 %all_gather.10 = bf16[128,3072]{0,1:T(8,128)(2,1)S(1)} all-gather(bf16[128,768]{0,1:T(8,128)(2,1)S(1)} %convert_element_type.17), channel_id=1, replica_groups=mesh['grp'=2,'col'=4,'row'=2,'dir'=2] {'row','dir'}, dimensions={1}, use_global_device_ids=true | all-gather | bytes 983040 | tf_op jit(solution)/shard_map/all_gather | solution.py:68
  102.6 114.2 %gather_fusion.1 = bf16[32768,128]{1,0:T(8,128)(2,1)} fusion(bf16[128,3072]{0,1:T(8,128)(2,1)S(1)} %all_gather.10, s32[32768]{0:T(1024)S(1)} %broadcast_clamp_fusion), kind=kCustom, calls=%fused_computation.1 | custom fusion | bytes 16908288 | tf_op jit(solution)/shard_map/jit(_take)/gather | solution.py:75
  216.8 13.4 %multiply_reduce_fusion = bf16[128,2048]{0,1:T(8,128)(2,1)} fusion(f32[4,4,2048]{2,1,0:T(4,128)S(1)} %bitcast.54, bf16[128,4,4,2048]{0,3,2,1:T(8,128)(2,1)} %bitcast.50, pred[4,4,2048]{2,1,0:T(4,128)(4,1)S(1)} %compare_and_fusion), kind=kLoop, calls=%fused_computation.2 | loop fusion | flops 16515072 | bytes 9076736 | tf_op jit(solution)/shard_map/reduce_sum | solution.py:79
  230.2 44.8 %all-gather.5.cloned.1.call-done = bf16[512,2048]{0,1:T(8,128)(2,1)} async-done(((bf16[128,2048]{0,1:T(8,128)(2,1)}), bf16[512,2048]{0,1:T(8,128)(2,1)}) %all-gather.5.cloned.1.call-update) | async-done | bytes 2097168 | tf_op jit(solution)/shard_map/all_gather | solution.py:81
  275.0 6.1 %fusion.3 = bf16[1,512,1024]{2,1,0:T(8,128)(2,1)} fusion(bf16[512,2048]{0,1:T(8,128)(2,1)} %all-gather.5.cloned.1.call-done, bf16[2048,1024]{1,0:T(8,128)(2,1)} %param.15), kind=kOutput, calls=%fused_computation.12 | convolution fusion | flops 2148007936 | bytes 7340032 | tf_op jit(solution)/shard_map/dot_general | solution.py:80
  (18 shorter events, 0.2 us)
Async XLA Ops:
  6.5 37.3 %copy-start = (bf16[3,4,256,256]{3,2,1,0:T(8,128)(2,1)S(1)}, bf16[3,4,256,256]{3,2,1,0:T(8,128)(2,1)}, u32[]{:S(2)}) copy-start(bf16[3,4,256,256]{3,2,1,0:T(8,128)(2,1)} %param.10) | copy-start | bytes 4718596
  6.5 33.1 %all-gather.3.cloned.1.call-start = ((), (), s32[]{:S(2)}) async-start(), calls=%async_computation.1 | async-start | bytes 1310720 | tf_op jit(solution)/shard_map/all_gather | solution.py:46
  8.5 84.5 %reduce-scatter.2.cloned.1.call-start = ((), (), s32[]{:S(2)}) async-start(), calls=%async_computation.2 | async-start | bytes 1966080 | tf_op jit(solution)/shard_map/reduce_scatter | solution.py:62
  41.8 6.9 %collective-permute-start = (bf16[128,4,256]{2,0,1:T(8,128)(2,1)S(1)}, bf16[128,4,256]{2,0,1:T(8,128)(2,1)S(1)}, u32[]{:S(2)}, u32[]{:S(2)}) collective-permute-start(bf16[128,4,256]{2,0,1:T(8,128)(2,1)S(1)} %fusion.8), channel_id=1, source_target_pairs={{0,1},{1,2},{2,3},{3,0},{4,5},{5,6},{6,7},{7,4},{8,9},{9,10},{10,1... | collective-permute-start | bytes 786440 | tf_op jit(solution)/shard_map/ppermute | solution.py:13
  41.9 7.6 %collective-permute-start.1 = (bf16[128,4,256]{2,0,1:T(8,128)(2,1)S(1)}, bf16[128,4,256]{2,0,1:T(8,128)(2,1)S(1)}, u32[]{:S(2)}, u32[]{:S(2)}) collective-permute-start(bf16[128,4,256]{2,0,1:T(8,128)(2,1)S(1)} %fusion.8), channel_id=1, source_target_pairs={{1,0},{2,1},{3,2},{0,3},{5,4},{6,5},{7,6},{4,7},{9,8},{10,9},{11,1... | collective-permute-start | bytes 786440 | tf_op jit(solution)/shard_map/ppermute | solution.py:13
  48.7 5.8 %collective-permute-start.2 = (bf16[128,4,256]{2,0,1:T(8,128)(2,1)S(1)}, bf16[128,4,256]{2,0,1:T(8,128)(2,1)S(1)}, u32[]{:S(2)}, u32[]{:S(2)}) collective-permute-start(bf16[128,4,256]{2,0,1:T(8,128)(2,1)S(1)} %collective-permute-done), channel_id=1, source_target_pairs={{0,1},{1,2},{2,3},{3,0},{4,5},{5,6},{6,7},{7,4},{8,9},{9,10},{10,1... | collective-permute-start | bytes 786440 | tf_op jit(solution)/shard_map/ppermute | solution.py:28
  49.1 5.8 %copy-start.3 = (bf16[3,4,256,256]{3,2,1,0:T(8,128)(2,1)S(1)}, bf16[3,4,256,256]{3,2,1,0:T(8,128)(2,1)}, u32[]{:S(2)}) copy-start(bf16[3,4,256,256]{3,2,1,0:T(8,128)(2,1)} %param.9) | copy-start | bytes 4718596
  54.9 2.4 copy-start.1
  57.1 217.9 %all-gather.5.cloned.1.call-start = ((), (), s32[]{:S(2)}) async-start(), calls=%async_computation.3 | async-start | bytes 2621440 | tf_op jit(solution)/shard_map/all_gather | solution.py:81
  102.6 114.2 %copy-start.2 = (f32[1,4,4,2048]{3,2,1,0:T(4,128)S(1)}, f32[1,4,4,2048]{3,2,1,0:T(4,128)}, u32[]{:S(2)}) copy-start(f32[1,4,4,2048]{3,2,1,0:T(4,128)} %param.14) | copy-start | bytes 393220
Sparse Core Ops, SparseCore 0:
  8.9 30.6 all-gather.2
  57.2 35.6 reduce-scatter.1
  230.3 44.6 all-gather.4
